TPU v7x, 128 devices: a whole 4x4x4 slice. The times are simulated.
128 devices in a mesh: rep: 1, dp: 128 (over x, y, z, core).
Axes of the slice: x: 4, y: 4, z: 4, core: 2. Of those that a mesh axis runs over, the one named last changes fastest.
Arguments:
- x: bfloat16 [128, 1024, 896], P(('rep', 'dp'))
- dy: bfloat16 [128, 1024, 896], P(('rep', 'dp'))
- w_gate: bfloat16 [2, 896, 2560], replicated
- w_up: bfloat16 [2, 896, 2560], replicated
- w_down: bfloat16 [2, 2560, 896], replicated
- m_w_gate: float32 [2, 896, 2560], P(None, 'dp')
- m_w_up: float32 [2, 896, 2560], P(None, 'dp')
- m_w_down: float32 [2, 2560, 896], P(None, 'dp')
- v_w_gate: float32 [2, 896, 2560], P(None, 'dp')
- v_w_up: float32 [2, 896, 2560], P(None, 'dp')
- v_w_down: float32 [2, 2560, 896], P(None, 'dp')
Outputs:
- output 1: bfloat16 [2, 896, 2560], P('rep')
- output 2: bfloat16 [2, 896, 2560], P('rep')
- output 3: bfloat16 [2, 2560, 896], P('rep')
- output 4: float32 [2, 896, 2560], P('rep', 'dp')
- output 5: float32 [2, 896, 2560], P('rep', 'dp')
- output 6: float32 [2, 2560, 896], P('rep', 'dp')
- output 7: float32 [2, 896, 2560], P('rep', 'dp')
- output 8: float32 [2, 896, 2560], P('rep', 'dp')
- output 9: float32 [2, 2560, 896], P('rep', 'dp')
All inputs are finite; a program needn't handle non-finite values.
Results may differ from a plain program's by a relative error of at most 0.022.
Values are sent between devices in bfloat16 or wider.
A program may use at most 1.5 GiB of HBM per device.

v0:
```python
import jax
import jax.numpy as jnp
from jax import lax

NAMES = ("w_gate", "w_up", "w_down")


def matmul(a, w):
    return jnp.dot(a, w, preferred_element_type=jnp.float32).astype(jnp.bfloat16)


def normed(h):
    wide = h.astype(jnp.float32)
    scale = lax.rsqrt(jnp.mean(wide**2, -1, keepdims=True) + 1e-6)
    return (wide * scale).astype(jnp.bfloat16)


def layer(h, w):
    a = normed(h)
    gate = jnp.dot(a, w["w_gate"], preferred_element_type=jnp.float32)
    up = jnp.dot(a, w["w_up"], preferred_element_type=jnp.float32)
    return h + matmul((jax.nn.silu(gate) * up).astype(jnp.bfloat16), w["w_down"])


def adamw(w, m, v, g):
    m = 0.9 * m + 0.1 * g
    v = 0.95 * v + 0.05 * g * g
    step = m * lax.rsqrt(v + 1e-8) + 0.1 * w
    return (w - 0.02 * step).astype(jnp.bfloat16), m, v


def clipped(gradients, sum_of_squares, count):
    factor = jnp.minimum(1.0, 0.5 * lax.rsqrt(sum_of_squares / count + 1e-30))
    return [g * factor for g in gradients]


def stack(weights, h):
    for number in range(weights["w_gate"].shape[0]):
        h = layer(h, {name: w[number] for name, w in weights.items()})
    return h


def solution(mesh):
    groups = mesh.shape["rep"]

    def step(x, dy, *arrays):
        weights, m, v = (arrays[i : i + 3] for i in (0, 3, 6))
        x, dy = (t.reshape(groups, -1, *t.shape[1:]) for t in (x, dy))

        def of_a_group(x, dy):
            _, back = jax.vjp(lambda w: stack(w, x), dict(zip(NAMES, weights, strict=True)))
            by_weights = back(dy)[0]
            gradients = [by_weights[name].astype(jnp.float32) for name in NAMES]
            gradients = clipped(gradients, sum(jnp.sum(g * g) for g in gradients), sum(g.size for g in gradients))
            new = [adamw(w.astype(jnp.float32), m, v, g) for w, m, v, g in zip(weights, m, v, gradients, strict=True)]
            return tuple(one[which] for which in range(3) for one in new)

        return tuple(t.reshape(-1, *t.shape[2:]) for t in jax.vmap(of_a_group)(x, dy))

    return step
```

profile of v0, /device:TPU:1, one launch (start us, length us, event | category | flops | bytes accessed | tf_op | source)
XLA Modules:
  0.0 1250.7 jit_solution(16264731688969451272)
XLA Ops:
  15.5 10.1 convolution_convert_fusion.1
  25.6 7.6 fusion.51
  33.2 5.6 fusion.49
  46.1 10.7 fusion.67
  56.8 10.8 fusion.41
  67.6 13.2 %fusion.28 = bf16[1024,896]{0,1:T(8,128)(2,1)} fusion(bf16[1024,2560]{1,0:T(8,128)(2,1)} %convolution_convert_fusion.1, f32[1024,2560]{1,0:T(8,128)} %fusion.41, bf16[2,896,2560]{2,1,0:T(8,128)(2,1)} %param.5), kind=kOutput, calls=%fused_computation.34 | convolution fusion | flops 4713349120 | bytes 22151168 | tf_op jit(solution)/vmap(transpose(jvp()))/dot_general | solution.py:21
  80.8 14.3 %fusion.26 = f32[2560,896]{0,1:T(8,128)} fusion(bf16[1024,2560]{1,0:T(8,128)(2,1)} %convolution_convert_fusion.1, f32[1024,2560]{1,0:T(8,128)} %fusion.41, bf16[1,1024,896]{1,2,0:T(8,128)(2,1)S(1)} %copy-done.10, f32[1024]{0:T(1024)S(1)} %bitcast.315), kind=kOutput, calls=%fused_computation.33 | convolution fusion | flops 4716101632 | bytes 26742784 | tf_op jit(solution)/vmap(transpose(jvp()))/dot_general | solution.py:21
  95.1 10.8 fusion.44
  105.9 9.2 fusion.10
  115.1 9.9 fusion.81
  125.0 7.6 fusion.69
  135.3 9.9 convolution_convert_fusion
  145.2 12.7 %fusion.14 = f32[2560,896]{0,1:T(8,128)} fusion(f32[1024,2560]{1,0:T(8,128)S(1)} %fusion.51, f32[1024,2560]{1,0:T(8,128)} %copy-done, bf16[1024,2560]{1,0:T(8,128)(2,1)} %convolution_convert_fusion, bf16[1,1024,896]{2,1,0:T(8,128)(2,1)S(1)} %copy-done.2, f32[1024]{0:T(1024)S(1)} %add_rsqrt_fusion), kind=kOutput, calls=%fused_computation.15 | convolution fusion | flops 4729208832 | bytes 37228544 | tf_op jit(solution)/vmap(transpose(jvp()))/dot_general | solution.py:20
  157.9 11.3 fusion.6
  169.2 412.5 %fusion.133 = (f32[2560,8]{0,1:T(8,128)S(1)}, f32[2560,8]{0,1:T(8,128)S(1)}, f32[2560,8]{0,1:T(8,128)S(1)}, f32[2560,8]{0,1:T(8,128)S(1)}) fusion(f32[2560,896]{0,1:T(8,128)} %fusion.14, f32[2560,896]{0,1:T(8,128)} %fusion.81, f32[2560,896]{0,1:T(8,128)} %fusion.6, f32[2560,896]{0,1:T(8,128)} %fusion.26), kind=kCustom, calls=%all-reduce-scatter.4 | all-reduce-scatter fusion | flops 10485761 | bytes 37027840
  592.2 12.8 %collective-permute-start.37 = (bf16[2560,8]{0,1:T(8,128)(2,1)S(1)}, bf16[2560,8]{0,1:T(8,128)(2,1)S(1)}, u32[]{:S(2)}, u32[]{:S(2)}) collective-permute-start(bf16[2560,8]{0,1:T(8,128)(2,1)S(1)} %convert.153), channel_id=1, source_target_pairs={{0,6},{1,7},{2,8},{3,9},{4,10},{5,11},{6,12},{7,13},{8,14},{9,15},... | collective-permute-start | bytes 122888
  611.3 19.4 %collective-permute-start.42 = (bf16[2560,8]{0,1:T(8,128)(2,1)S(1)}, bf16[2560,8]{0,1:T(8,128)(2,1)S(1)}, u32[]{:S(2)}, u32[]{:S(2)}) collective-permute-start(bf16[2560,8]{0,1:T(8,128)(2,1)S(1)} %convert.153), channel_id=1, source_target_pairs={{0,11},{1,12},{2,13},{3,14},{4,15},{5,16},{6,17},{7,18},{8,19},{9,... | collective-permute-start | bytes 122888
  673.1 12.4 fusion.32
  696.3 8.2 fusion.138
  713.3 4.3 collective-permute-start.4
  719.0 132.8 %all-reduce.24 = (bf16[896,2560]{0,1:T(8,128)(2,1)}, bf16[2560,896]{1,0:T(8,128)(2,1)}) all-reduce(f32[896,2560]{0,1:T(8,128)} %fusion.138, f32[2560,896]{1,0:T(8,128)} %fusion.32), channel_id=21, replica_groups=mesh['axis_0'=128] {'axis_0'}, use_global_device_ids=true, to_apply=%add.5.clone.clone | all-reduce | flops 4587520 | bytes 27525120
  874.8 6.9 collective-permute-start.12
  883.6 6.5 collective-permute-start.14
  915.7 6.1 collective-permute-start.22
  930.4 11.0 concatenate
  960.1 62.7 %all-reduce.10 = f32[]{:T(128)} all-reduce(f32[]{:T(128)S(6)} %add.102), channel_id=3, replica_groups=mesh['rep'=1,'dp'=128] {'dp'}, use_global_device_ids=true, to_apply=%region_3.4.clone | all-reduce | flops 1 | bytes 8 | tf_op jit(solution)/vmap()/reduce_sum | solution.py:54
  1033.8 59.4 %all-gather.10.cloned.1.call-done = bf16[1,2,896,2560]{3,1,0,2:T(2,128)(2,1)} async-done(((bf16[1,2,7,2560]{3,1,0,2:T(2,128)(2,1)}), bf16[1,2,896,2560]{3,1,0,2:T(2,128)(2,1)}) %all-gather.10.cloned.1.call-update) | async-done | bytes 9175056 | tf_op jit(solution)/reshape | solution.py:58
  1093.2 8.7 copy.25
  1101.9 62.8 %all-gather.12.cloned.1.call-done = bf16[1,2,896,2560]{3,1,0,2:T(2,128)(2,1)} async-done(((bf16[1,2,7,2560]{3,1,0,2:T(2,128)(2,1)}), bf16[1,2,896,2560]{3,1,0,2:T(2,128)(2,1)}) %all-gather.12.cloned.1.call-update) | async-done | bytes 9175056 | tf_op jit(solution)/reshape | solution.py:58
  1164.6 8.7 copy.26
  1173.3 62.2 %all-gather.14.cloned.1.call-done = bf16[1,2,2560,896]{3,1,0,2:T(2,128)(2,1)} async-done(((bf16[1,2,20,896]{3,1,0,2:T(2,128)(2,1)}), bf16[1,2,2560,896]{3,1,0,2:T(2,128)(2,1)}) %all-gather.14.cloned.1.call-update) | async-done | bytes 9175056 | tf_op jit(solution)/reshape | solution.py:58
  1235.5 8.4 copy.27
  (241 shorter events, 183.3 us)
Async XLA Ops:
  7.2 1086.0 %all-gather.10.cloned.1.call-start = ((), (), s32[]{:S(2)}) async-start(), calls=%async_computation | async-start | bytes 9246720 | tf_op jit(solution)/reshape | solution.py:58
  605.0 25.6 %collective-permute-start.38 = (bf16[2560,8]{0,1:T(8,128)(2,1)S(1)}, bf16[2560,8]{0,1:T(8,128)(2,1)S(1)}, u32[]{:S(2)}, u32[]{:S(2)}) collective-permute-start(bf16[2560,8]{0,1:T(8,128)(2,1)S(1)} %convert.153), channel_id=1, source_target_pairs={{0,7},{1,8},{2,9},{3,10},{4,11},{5,12},{6,13},{7,14},{8,15},{9,16}... | collective-permute-start | bytes 122888
  607.0 27.4 %collective-permute-start.39 = (bf16[2560,8]{0,1:T(8,128)(2,1)S(1)}, bf16[2560,8]{0,1:T(8,128)(2,1)S(1)}, u32[]{:S(2)}, u32[]{:S(2)}) collective-permute-start(bf16[2560,8]{0,1:T(8,128)(2,1)S(1)} %convert.153), channel_id=1, source_target_pairs={{0,8},{1,9},{2,10},{3,11},{4,12},{5,13},{6,14},{7,15},{8,16},{9,17... | collective-permute-start | bytes 122888
  608.6 29.2 %collective-permute-start.40 = (bf16[2560,8]{0,1:T(8,128)(2,1)S(1)}, bf16[2560,8]{0,1:T(8,128)(2,1)S(1)}, u32[]{:S(2)}, u32[]{:S(2)}) collective-permute-start(bf16[2560,8]{0,1:T(8,128)(2,1)S(1)} %convert.153), channel_id=1, source_target_pairs={{0,9},{1,10},{2,11},{3,12},{4,13},{5,14},{6,15},{7,16},{8,17},{9,1... | collective-permute-start | bytes 122888
  609.9 30.1 %collective-permute-start.41 = (bf16[2560,8]{0,1:T(8,128)(2,1)S(1)}, bf16[2560,8]{0,1:T(8,128)(2,1)S(1)}, u32[]{:S(2)}, u32[]{:S(2)}) collective-permute-start(bf16[2560,8]{0,1:T(8,128)(2,1)S(1)} %convert.153), channel_id=1, source_target_pairs={{0,10},{1,11},{2,12},{3,13},{4,14},{5,15},{6,16},{7,17},{8,18},{9,... | collective-permute-start | bytes 122888
  611.3 32.8 %collective-permute-start.42 = (bf16[2560,8]{0,1:T(8,128)(2,1)S(1)}, bf16[2560,8]{0,1:T(8,128)(2,1)S(1)}, u32[]{:S(2)}, u32[]{:S(2)}) collective-permute-start(bf16[2560,8]{0,1:T(8,128)(2,1)S(1)} %convert.153), channel_id=1, source_target_pairs={{0,11},{1,12},{2,13},{3,14},{4,15},{5,16},{6,17},{7,18},{8,19},{9,... | collective-permute-start | bytes 122888
  661.0 24.5 %collective-permute-start.54 = (bf16[2560,8]{0,1:T(8,128)(2,1)S(1)}, bf16[2560,8]{0,1:T(8,128)(2,1)S(1)}, u32[]{:S(2)}, u32[]{:S(2)}) collective-permute-start(bf16[2560,8]{0,1:T(8,128)(2,1)S(1)} %convert.154), channel_id=1, source_target_pairs={{0,7},{1,8},{2,9},{3,10},{4,11},{5,12},{6,13},{7,14},{8,15},{9,16}... | collective-permute-start | bytes 122888
  664.7 22.7 %collective-permute-start.55 = (bf16[2560,8]{0,1:T(8,128)(2,1)S(1)}, bf16[2560,8]{0,1:T(8,128)(2,1)S(1)}, u32[]{:S(2)}, u32[]{:S(2)}) collective-permute-start(bf16[2560,8]{0,1:T(8,128)(2,1)S(1)} %convert.154), channel_id=1, source_target_pairs={{0,8},{1,9},{2,10},{3,11},{4,12},{5,13},{6,14},{7,15},{8,16},{9,17... | collective-permute-start | bytes 122888
  666.4 23.0 %collective-permute-start.56 = (bf16[2560,8]{0,1:T(8,128)(2,1)S(1)}, bf16[2560,8]{0,1:T(8,128)(2,1)S(1)}, u32[]{:S(2)}, u32[]{:S(2)}) collective-permute-start(bf16[2560,8]{0,1:T(8,128)(2,1)S(1)} %convert.154), channel_id=1, source_target_pairs={{0,9},{1,10},{2,11},{3,12},{4,13},{5,14},{6,15},{7,16},{8,17},{9,1... | collective-permute-start | bytes 122888
  668.6 23.5 %collective-permute-start.57 = (bf16[2560,8]{0,1:T(8,128)(2,1)S(1)}, bf16[2560,8]{0,1:T(8,128)(2,1)S(1)}, u32[]{:S(2)}, u32[]{:S(2)}) collective-permute-start(bf16[2560,8]{0,1:T(8,128)(2,1)S(1)} %convert.154), channel_id=1, source_target_pairs={{0,10},{1,11},{2,12},{3,13},{4,14},{5,15},{6,16},{7,17},{8,18},{9,... | collective-permute-start | bytes 122888
  670.2 23.1 %collective-permute-start.58 = (bf16[2560,8]{0,1:T(8,128)(2,1)S(1)}, bf16[2560,8]{0,1:T(8,128)(2,1)S(1)}, u32[]{:S(2)}, u32[]{:S(2)}) collective-permute-start(bf16[2560,8]{0,1:T(8,128)(2,1)S(1)} %convert.154), channel_id=1, source_target_pairs={{0,11},{1,12},{2,13},{3,14},{4,15},{5,16},{6,17},{7,18},{8,19},{9,... | collective-permute-start | bytes 122888
  692.1 21.2 %collective-permute-start.62 = (bf16[2560,8]{0,1:T(8,128)(2,1)S(1)}, bf16[2560,8]{0,1:T(8,128)(2,1)S(1)}, u32[]{:S(2)}, u32[]{:S(2)}) collective-permute-start(bf16[2560,8]{0,1:T(8,128)(2,1)S(1)} %convert.154), channel_id=1, source_target_pairs={{0,15},{1,16},{2,17},{3,18},{4,19},{5,20},{6,21},{7,22},{8,23},{9,... | collective-permute-start | bytes 122888
  693.4 24.2 %collective-permute-start.48 = (bf16[2560,8]{0,1:T(8,128)(2,1)S(1)}, bf16[2560,8]{0,1:T(8,128)(2,1)}, u32[]{:S(2)}, u32[]{:S(2)}) collective-permute-start(bf16[2560,8]{0,1:T(8,128)(2,1)S(1)} %convert.154), channel_id=1, source_target_pairs={{0,1},{1,2},{2,3},{3,4},{4,5},{5,6},{6,7},{7,8},{8,9},{9,10},{10,1... | collective-permute-start | bytes 122888
  705.0 146.7 %collective-permute-start.1 = (bf16[2560,8]{0,1:T(8,128)(2,1)}, bf16[2560,8]{0,1:T(8,128)(2,1)S(1)}, u32[]{:S(2)}, u32[]{:S(2)}) collective-permute-start(bf16[2560,8]{0,1:T(8,128)(2,1)} %convert.155), channel_id=1, source_target_pairs={{0,2},{1,3},{2,4},{3,5},{4,6},{5,7},{6,8},{7,9},{8,10},{9,11},{10,... | collective-permute-start | bytes 122888
  707.0 148.7 %collective-permute-start.2 = (bf16[2560,8]{0,1:T(8,128)(2,1)}, bf16[2560,8]{0,1:T(8,128)(2,1)S(1)}, u32[]{:S(2)}, u32[]{:S(2)}) collective-permute-start(bf16[2560,8]{0,1:T(8,128)(2,1)} %convert.155), channel_id=1, source_target_pairs={{0,3},{1,4},{2,5},{3,6},{4,7},{5,8},{6,9},{7,10},{8,11},{9,12},{10... | collective-permute-start | bytes 122888
  710.1 148.2 %collective-permute-start.3 = (bf16[2560,8]{0,1:T(8,128)(2,1)}, bf16[2560,8]{0,1:T(8,128)(2,1)S(1)}, u32[]{:S(2)}, u32[]{:S(2)}) collective-permute-start(bf16[2560,8]{0,1:T(8,128)(2,1)} %convert.155), channel_id=1, source_target_pairs={{0,4},{1,5},{2,6},{3,7},{4,8},{5,9},{6,10},{7,11},{8,12},{9,13},{1... | collective-permute-start | bytes 122888
  713.3 148.7 %collective-permute-start.4 = (bf16[2560,8]{0,1:T(8,128)(2,1)}, bf16[2560,8]{0,1:T(8,128)(2,1)S(1)}, u32[]{:S(2)}, u32[]{:S(2)}) collective-permute-start(bf16[2560,8]{0,1:T(8,128)(2,1)} %convert.155), channel_id=1, source_target_pairs={{0,5},{1,6},{2,7},{3,8},{4,9},{5,10},{6,11},{7,12},{8,13},{9,14},{... | collective-permute-start | bytes 122888
  717.6 148.2 %collective-permute-start.5 = (bf16[2560,8]{0,1:T(8,128)(2,1)}, bf16[2560,8]{0,1:T(8,128)(2,1)S(1)}, u32[]{:S(2)}, u32[]{:S(2)}) collective-permute-start(bf16[2560,8]{0,1:T(8,128)(2,1)} %convert.155), channel_id=1, source_target_pairs={{0,6},{1,7},{2,8},{3,9},{4,10},{5,11},{6,12},{7,13},{8,14},{9,15},... | collective-permute-start | bytes 122888
  858.3 23.4 %collective-permute-start.8 = (bf16[2560,8]{0,1:T(8,128)(2,1)}, bf16[2560,8]{0,1:T(8,128)(2,1)S(1)}, u32[]{:S(2)}, u32[]{:S(2)}) collective-permute-start(bf16[2560,8]{0,1:T(8,128)(2,1)} %convert.155), channel_id=1, source_target_pairs={{0,9},{1,10},{2,11},{3,12},{4,13},{5,14},{6,15},{7,16},{8,17},{9,1... | collective-permute-start | bytes 122888
  861.9 21.7 %collective-permute-start.9 = (bf16[2560,8]{0,1:T(8,128)(2,1)}, bf16[2560,8]{0,1:T(8,128)(2,1)S(1)}, u32[]{:S(2)}, u32[]{:S(2)}) collective-permute-start(bf16[2560,8]{0,1:T(8,128)(2,1)} %convert.155), channel_id=1, source_target_pairs={{0,10},{1,11},{2,12},{3,13},{4,14},{5,15},{6,16},{7,17},{8,18},{9,... | collective-permute-start | bytes 122888
  865.8 24.4 %collective-permute-start.10 = (bf16[2560,8]{0,1:T(8,128)(2,1)}, bf16[2560,8]{0,1:T(8,128)(2,1)S(1)}, u32[]{:S(2)}, u32[]{:S(2)}) collective-permute-start(bf16[2560,8]{0,1:T(8,128)(2,1)} %convert.155), channel_id=1, source_target_pairs={{0,11},{1,12},{2,13},{3,14},{4,15},{5,16},{6,17},{7,18},{8,19},{9,... | collective-permute-start | bytes 122888
  870.6 26.2 %collective-permute-start.11 = (bf16[2560,8]{0,1:T(8,128)(2,1)}, bf16[2560,8]{0,1:T(8,128)(2,1)}, u32[]{:S(2)}, u32[]{:S(2)}) collective-permute-start(bf16[2560,8]{0,1:T(8,128)(2,1)} %convert.155), channel_id=1, source_target_pairs={{0,12},{1,13},{2,14},{3,15},{4,16},{5,17},{6,18},{7,19},{8,20},{9,... | collective-permute-start | bytes 122888
  874.8 26.2 %collective-permute-start.12 = (bf16[2560,8]{0,1:T(8,128)(2,1)}, bf16[2560,8]{0,1:T(8,128)(2,1)}, u32[]{:S(2)}, u32[]{:S(2)}) collective-permute-start(bf16[2560,8]{0,1:T(8,128)(2,1)} %convert.155), channel_id=1, source_target_pairs={{0,13},{1,14},{2,15},{3,16},{4,17},{5,18},{6,19},{7,20},{8,21},{9,... | collective-permute-start | bytes 122888
  881.7 22.1 %collective-permute-start.13 = (bf16[2560,8]{0,1:T(8,128)(2,1)}, bf16[2560,8]{0,1:T(8,128)(2,1)}, u32[]{:S(2)}, u32[]{:S(2)}) collective-permute-start(bf16[2560,8]{0,1:T(8,128)(2,1)} %convert.155), channel_id=1, source_target_pairs={{0,14},{1,15},{2,16},{3,17},{4,18},{5,19},{6,20},{7,21},{8,22},{9,... | collective-permute-start | bytes 122888
  883.6 22.6 %collective-permute-start.14 = (bf16[2560,8]{0,1:T(8,128)(2,1)}, bf16[2560,8]{0,1:T(8,128)(2,1)}, u32[]{:S(2)}, u32[]{:S(2)}) collective-permute-start(bf16[2560,8]{0,1:T(8,128)(2,1)} %convert.155), channel_id=1, source_target_pairs={{0,15},{1,16},{2,17},{3,18},{4,19},{5,20},{6,21},{7,22},{8,23},{9,... | collective-permute-start | bytes 122888
  915.7 25.7 %collective-permute-start.22 = (bf16[2560,8]{0,1:T(8,128)(2,1)}, bf16[2560,8]{0,1:T(8,128)(2,1)S(1)}, u32[]{:S(2)}, u32[]{:S(2)}) collective-permute-start(bf16[2560,8]{0,1:T(8,128)(2,1)} %convert.156), channel_id=1, source_target_pairs={{0,7},{1,8},{2,9},{3,10},{4,11},{5,12},{6,13},{7,14},{8,15},{9,16}... | collective-permute-start | bytes 122888
  921.8 22.8 %collective-permute-start.23 = (bf16[2560,8]{0,1:T(8,128)(2,1)}, bf16[2560,8]{0,1:T(8,128)(2,1)S(1)}, u32[]{:S(2)}, u32[]{:S(2)}) collective-permute-start(bf16[2560,8]{0,1:T(8,128)(2,1)} %convert.156), channel_id=1, source_target_pairs={{0,8},{1,9},{2,10},{3,11},{4,12},{5,13},{6,14},{7,15},{8,16},{9,17... | collective-permute-start | bytes 122888
  923.1 23.7 %collective-permute-start.24 = (bf16[2560,8]{0,1:T(8,128)(2,1)}, bf16[2560,8]{0,1:T(8,128)(2,1)S(1)}, u32[]{:S(2)}, u32[]{:S(2)}) collective-permute-start(bf16[2560,8]{0,1:T(8,128)(2,1)} %convert.156), channel_id=1, source_target_pairs={{0,9},{1,10},{2,11},{3,12},{4,13},{5,14},{6,15},{7,16},{8,17},{9,1... | collective-permute-start | bytes 122888
  925.2 24.6 %collective-permute-start.25 = (bf16[2560,8]{0,1:T(8,128)(2,1)}, bf16[2560,8]{0,1:T(8,128)(2,1)S(1)}, u32[]{:S(2)}, u32[]{:S(2)}) collective-permute-start(bf16[2560,8]{0,1:T(8,128)(2,1)} %convert.156), channel_id=1, source_target_pairs={{0,10},{1,11},{2,12},{3,13},{4,14},{5,15},{6,16},{7,17},{8,18},{9,... | collective-permute-start | bytes 122888
  928.5 22.6 %collective-permute-start.26 = (bf16[2560,8]{0,1:T(8,128)(2,1)}, bf16[2560,8]{0,1:T(8,128)(2,1)S(1)}, u32[]{:S(2)}, u32[]{:S(2)}) collective-permute-start(bf16[2560,8]{0,1:T(8,128)(2,1)} %convert.156), channel_id=1, source_target_pairs={{0,11},{1,12},{2,13},{3,14},{4,15},{5,16},{6,17},{7,18},{8,19},{9,... | collective-permute-start | bytes 122888
  1025.4 139.3 %all-gather.12.cloned.1.call-start = ((), (), s32[]{:S(2)}) async-start(), calls=%async_computation.1 | async-start | bytes 9246720 | tf_op jit(solution)/reshape | solution.py:58
  1027.2 208.3 %all-gather.14.cloned.1.call-start = ((), (), s32[]{:S(2)}) async-start(), calls=%async_computation.2 | async-start | bytes 9246720 | tf_op jit(solution)/reshape | solution.py:58
  (70 other events, 2905.0 us)
Sparse Core Ops, SparseCore 0:
  1025.5 67.6 all-gather.9
  1096.8 67.7 all-gather.11
  1167.7 67.7 all-gather.13
where the time goes:
time: 1260 us; the launch traced here: 1250 us
  blocking collectives  608 us (48%)
  starting transfers between devices  197 us (16%)
  waiting for transfers between devices  186 us (15%)
  matrix products  155 us (12%)
  local copies, waits for them, and re-layouts  65.1 us (5%)
  other arithmetic  21.7 us (2%)
  between operations  18.1 us (1%)
    unnamed x2, blocking collectives  545 us
    unnamed x64, starting transfers between devices  197 us
    reshape x3, waiting for transfers between devices, step(): t.reshape(-1, *t.shape[2:])  184 us
    reduce_sum x1, blocking collectives, of_a_group(): jnp.sum(g * g)  62.7 us
    unnamed x89, local copies, waits for them, and re-layouts  61.2 us
    dot_general x5, matrix products, layer(): up = jnp.dot(a, w['w_up'], preferred_element_type=jnp.float32)  55.2 us
    dot_general x5, matrix products, matmul(): jnp.dot(a, w, preferred_element_type=jnp.float32).astype(jnp.bfloat16)  51.1 us
    dot_general x5, matrix products, layer(): gate = jnp.dot(a, w['w_gate'], preferred_element_type=jnp.float32)  48.6 us
  transfers between devices with their start and end apart: 67, of which 4 were waited for; matrix products, arithmetic and copies ran while one was open for 5% of the time, Pallas kernels for 0%

commit v1 on v0

v1 whole, which is shorter than its diff:
```python
import functools

import jax
import jax.numpy as jnp
from jax import lax
from jax.experimental import pallas as pl
from jax.experimental.pallas import tpu as pltpu
from jax.sharding import PartitionSpec as P

NAMES = ("w_gate", "w_up", "w_down")
F32, BF16 = jnp.float32, jnp.bfloat16
MESH = pl.DeviceIdType.MESH
STRIDE = {"x": 32, "y": 8, "z": 2}
ORDER = (("y", "z", "x"), ("z", "x", "y"), ("x", "y", "z"))
PAD = (8, 8, 32)
ROWS = (7, 7, 20)


def prod(ns):
    out = 1
    for n in ns:
        out *= n
    return out


def add(dst, *srcs):
    *lead, rows, _ = dst.shape
    steps = rows // 16

    def body(i, carry):
        q, index = i // steps, []
        for n in reversed(lead):
            index.append(q % n)
            q = q // n
        row = slice(None) if steps == 1 else pl.ds(pl.multiple_of((i % steps) * 16, 16), 16)
        at = (*reversed(index), row, slice(None))
        total = srcs[0][at].astype(F32)
        for s in srcs[1:]:
            total = total + s[at].astype(F32)
        dst[at] = total.astype(BF16)
        return carry

    lax.fori_loop(0, prod(lead) * steps, body, 0)


def step_kernel(count, *refs):
    it = iter(refs)

    def take(n):
        return [next(it) for _ in range(n)]

    grads = [take(2) for _ in range(3)]
    w_in, m_in, v_in = take(3), take(3), take(3)
    w_out, m_out, v_out = take(3), take(3), take(3)
    A, R0, R1, R2, R3, S3, R4, G, W5, R5, N = (take(3) for _ in range(11))
    T, n1, n2, n3 = take(4)
    p0s, p0r, p0l, p1s, p1r, p2s, p2r, p3s, p3r, nss, nrs, q3s, q3r, q2s, q2r, q1s, q1r, q0s, q0r, q0l = take(20)

    me = lax.axis_index("dp")
    core = me % 2
    co = {d: (me // s) % 4 for d, s in STRIDE.items()}
    partner = me + 1 - 2 * core
    WL = [(w, l) for w in range(3) for l in range(2)]
    started = []

    def near(dim, offset):
        return me + ((co[dim] + offset) % 4 - co[dim]) * STRIDE[dim]

    def remote(src, dst, ssem, rsem, device):
        return pltpu.make_async_remote_copy(
            src_ref=src, dst_ref=dst, send_sem=ssem, recv_sem=rsem, device_id={"dp": device}, device_id_type=MESH
        )

    def send(*args):
        copy = remote(*args)
        copy.start()
        started.append(copy)
        return copy

    def region(w, ref, k, c, half=None):
        if w == 0:
            return ref.at[pl.ds(2 * c, 2), k] if half is None else ref.at[pl.ds(2 * c + half, 1), k]
        if w == 1:
            return ref.at[:, pl.ds(2 * c, 2), k] if half is None else ref.at[pl.ds(2 * half, 2), pl.ds(2 * c, 2), k]
        return ref.at[k, :, c] if half is None else ref.at[k, pl.ds(2 * half, 2), c]

    def half_of(ref, h):
        n = ref.shape[0] // 2
        return ref.at[pl.ds(n * h, n)]

    def part(w, ref, j):
        return ref.at[:, j] if w == 0 else ref.at[j]

    peers = [partner]
    for d, s in STRIDE.items():
        for k in (1, 2, 3):
            other = near(d, k)
            peers += [other, other + 1 - 2 * core]
    barrier = pltpu.get_barrier_semaphore()
    for p in peers:
        pl.semaphore_signal(barrier, inc=1, device_id={"dp": p}, device_id_type=MESH)
    pl.semaphore_wait(barrier, len(peers))

    p0 = {}
    for oi, off in enumerate((2, 1, 3, 0)):
        for w, l in WL:
            k = (co[ORDER[w][0]] + off) % 4
            i = (oi * 3 + w) * 2 + l
            out = send(region(w, grads[w][l], k, 1 - core), R0[w].at[l, k], p0s.at[i], p0r.at[i], partner)
            own = pltpu.make_async_copy(region(w, grads[w][l], k, core), A[w].at[l, k], p0l.at[i])
            own.start()
            p0[off, w, l] = (out, own)

    def arrive(off, w, l):
        out, own = p0[off, w, l]
        own.wait()
        out.wait_recv()

    p1 = {}

    def p1_send(t, w, l, src, dst, offset):
        i = (w * 2 + l) * 6 + t
        p1[t, w, l] = send(src, dst, p1s.at[i], p1r.at[i], near(ORDER[w][0], offset))

    def blocks(w, l, off):
        k = (co[ORDER[w][0]] + off) % 4
        return A[w].at[l, k], R0[w].at[l, k]

    for w, l in WL:
        arrive(2, w, l)
        a, r = blocks(w, l, 2)
        add(a, a, r)
        p1_send(0, w, l, half_of(a, 0), R1[w].at[l, 0], 1)
        p1_send(1, w, l, half_of(a, 1), R1[w].at[l, 1], -1)
    for w, l in WL:
        arrive(1, w, l)
        a, r = (half_of(b, 1) for b in blocks(w, l, 1))
        add(a, a, r)
        p1_send(2, w, l, a, half_of(R2[w].at[l, 0], 1), 1)
        arrive(3, w, l)
        a, r = (half_of(b, 0) for b in blocks(w, l, 3))
        add(a, a, r)
        p1_send(3, w, l, a, half_of(R2[w].at[l, 1], 0), -1)
    for w, l in WL:
        p1[0, w, l].wait_recv()
        a, r = (half_of(b, 0) for b in blocks(w, l, 1))
        add(a, a, r, R1[w].at[l, 0])
        p1_send(4, w, l, a, half_of(R2[w].at[l, 0], 0), 1)
        p1[1, w, l].wait_recv()
        a, r = (half_of(b, 1) for b in blocks(w, l, 3))
        add(a, a, r, R1[w].at[l, 1])
        p1_send(5, w, l, a, half_of(R2[w].at[l, 1], 1), -1)
    p2 = {}
    for w, l in WL:
        arrive(0, w, l)
        for t in (2, 3, 4, 5):
            p1[t, w, l].wait_recv()
        a, r = blocks(w, l, 0)
        add(a, a, r, R2[w].at[l, 0], R2[w].at[l, 1])
        d2 = ORDER[w][1]
        for j in (1, 2, 3):
            i = (w * 2 + l) * 3 + j - 1
            p2[j, w, l] = send(
                part(w, a, (co[d2] + j) % 4), R3[w].at[l, j - 1], p2s.at[i], p2r.at[i], near(d2, j)
            )

    def exchange(w, l, e, c):
        d3 = ORDER[w][2]
        other = me + (2 * core + e - co[d3]) * STRIDE[d3] + c - core
        copy = remote(
            S3[w].at[l, e, c], R4[w].at[l, co[d3]], p3s.at[((w * 2 + l) * 2 + e) * 2 + c], p3r.at[(w * 2 + l) * 4 + co[d3]], other
        )
        return other, copy

    for w, l in WL:
        for j in (1, 2, 3):
            p2[j, w, l].wait_recv()
        own = part(w, blocks(w, l, 0)[0], co[ORDER[w][1]])
        terms = [own] + [R3[w].at[l, j] for j in range(3)]
        if w < 2:
            for e in range(2):
                total = sum((t[e].astype(F32) for t in terms[1:]), terms[0][e].astype(F32))
                for c in range(2):
                    S3[w][l, e, c] = total[8 * c : 8 * c + 8].astype(BF16)
        else:
            for r in range(5):
                rows = slice(16 * r, 16 * r + 16)
                T[rows] = sum((t[rows].astype(F32) for t in terms[1:]), terms[0][rows].astype(F32))
            for e in range(2):
                for c in range(2):
                    piece = T[40 * e + 20 * c : 40 * e + 20 * c + 20]
                    G[2][l, 0:20] = piece
                    G[2][l, 20:32] = jnp.zeros((12, piece.shape[1]), F32)
                    S3[2][l, e, c] = G[2][l].astype(BF16)
        for e in range(2):
            for c in range(2):
                other, copy = exchange(w, l, e, c)

                @pl.when(other != me)
                def _():
                    copy.start()

                @pl.when(other == me)
                def _():
                    R4[w][l, co[ORDER[w][2]]] = S3[w][l, e, c]

    squares = jnp.zeros((8, 128), F32)
    for w, l in WL:
        d3 = ORDER[w][2]
        for s in range(4):
            mine = (co[d3] == s) & (co[d3] // 2 == core)

            @pl.when(jnp.logical_not(mine))
            def _():
                remote(S3[w].at[l, 0, 0], R4[w].at[l, s], p3s.at[0], p3r.at[(w * 2 + l) * 4 + s], me).wait_recv()

        g = sum((R4[w][l, s].astype(F32) for s in range(1, 4)), R4[w][l, 0].astype(F32)).astype(BF16).astype(F32)
        G[w][l] = g
        sq = g * g
        for r in range(0, sq.shape[0], 8):
            for c in range(0, sq.shape[1], 128):
                squares = squares + sq[r : r + 8, c : c + 128]

    line = co["z"] * 2 + core
    n1[line] = squares
    copies = []
    for j in range(1, 8):
        other = me + (line + j) % 8 - line
        copies.append(send(n1.at[line], n1.at[line], nss.at[j - 1], nrs.at[j - 1], other))
    for copy in copies:
        copy.wait_recv()
    for base, ref, dim, before in ((7, n2, "y", n1), (10, n3, "x", n2)):
        total = before[0]
        for s in range(1, before.shape[0]):
            total = total + before[s]
        ref[co[dim]] = total
        copies = []
        for j in (1, 2, 3):
            i = base + j - 1
            copies.append(send(ref.at[co[dim]], ref.at[co[dim]], nss.at[i], nrs.at[i], near(dim, j)))
        for copy in copies:
            copy.wait_recv()
    total = n3[0] + n3[1] + n3[2] + n3[3]
    total = jnp.sum(jnp.sum(total, axis=0, keepdims=True), axis=1, keepdims=True)
    factor = jnp.minimum(1.0, 0.5 * lax.rsqrt(total * (1.0 / count) + 1e-30))

    def spread(w, l, k):
        d3 = ORDER[w][2]
        to = co[d3] // 2
        other = me + (k - co[d3]) * STRIDE[d3] + to - core
        slot = (co[d3] % 2) * 2 + core
        copy = remote(W5[w].at[l], R5[w].at[l, slot], q3s.at[(w * 2 + l) * 4 + k], q3r.at[(w * 2 + l) * 4 + slot], other)
        return other, slot, copy

    for w, l in WL:
        n = ROWS[w]
        g = G[w][l, 0:n] * factor
        m = 0.9 * m_in[w][l] + 0.1 * g
        v = 0.95 * v_in[w][l] + 0.05 * g * g
        m_out[w][l] = m
        v_out[w][l] = v
        old = w_in[w][l]
        G[w][l, 0:n] = old - 0.02 * (m * lax.rsqrt(v + 1e-8) + 0.1 * old)
        W5[w][l] = G[w][l].astype(BF16)
        for k in range(4):
            other, slot, copy = spread(w, l, k)

            @pl.when(other != me)
            def _():
                copy.start()

            @pl.when(other == me)
            def _():
                R5[w][l, slot] = W5[w][l]

    q2 = {}
    for w, l in WL:
        d2, d3 = ORDER[w][1:]
        for s in range(4):
            mine = (co[d3] // 2 == core) & ((co[d3] % 2) * 2 + core == s)

            @pl.when(jnp.logical_not(mine))
            def _():
                remote(W5[w].at[l], R5[w].at[l, s], q3s.at[0], q3r.at[(w * 2 + l) * 4 + s], me).wait_recv()

        block = part(w, N[w].at[l], co[d2])
        if w < 2:
            for e in range(2):
                both = [R5[w][l, 2 * e + c].astype(F32) for c in range(2)]
                block[e] = jnp.concatenate(both, axis=0).astype(BF16)
        else:
            for s in range(4):
                T[20 * s : 20 * s + 20] = R5[w][l, s].astype(F32)[0:20]
            for r in range(5):
                block[16 * r : 16 * r + 16] = T[16 * r : 16 * r + 16].astype(BF16)
        for j in (1, 2, 3):
            i = (w * 2 + l) * 3 + j - 1
            q2[j, w, l] = send(block, block, q2s.at[i], q2r.at[i], near(d2, j))

    q1, q0, local = {}, {}, []

    def q1_send(t, w, l, src, dst, offset):
        i = (w * 2 + l) * 4 + t
        q1[t, w, l] = send(src, dst, q1s.at[i], q1r.at[i], near(ORDER[w][0], offset))

    def q0_send(t, w, l, src, dst):
        i = (w * 2 + l) * 5 + t
        q0[t, w, l] = send(src, dst, q0s.at[i], q0r.at[i], partner)

    for w, l in WL:
        for j in (1, 2, 3):
            q2[j, w, l].wait_recv()
        here = region(w, w_out[w].at[l], co[ORDER[w][0]], core)
        q1_send(0, w, l, N[w].at[l], here, 1)
        q1_send(1, w, l, N[w].at[l], here, -1)
        q0_send(0, w, l, N[w].at[l], here)
        copy = pltpu.make_async_copy(N[w].at[l], here, q0l.at[w * 2 + l])
        copy.start()
        local.append(copy)
    for w, l in WL:
        d1 = ORDER[w][0]
        for t, off, h, to in ((0, 3, 0, 1), (1, 1, 1, -1)):
            q1[t, w, l].wait_recv()
            k = (co[d1] + off) % 4
            half = region(w, w_out[w].at[l], k, core, h)
            q1_send(2 + t, w, l, half, half, to)
            whole = region(w, w_out[w].at[l], k, core)
            q0_send(1 + t, w, l, whole, whole)
    for w, l in WL:
        for t in (0, 1):
            q1[2 + t, w, l].wait_recv()
            half = region(w, w_out[w].at[l], (co[ORDER[w][0]] + 2) % 4, core, t)
            q0_send(3 + t, w, l, half, half)
    for copy in q0.values():
        copy.wait_recv()
    for copy in local:
        copy.wait()
    for copy in started:
        copy.wait_send()
    for w, l in WL:
        for e in range(2):
            for c in range(2):
                other, copy = exchange(w, l, e, c)

                @pl.when(other != me)
                def _():
                    copy.wait_send()

        for k in range(4):
            other, _, copy = spread(w, l, k)

            @pl.when(other != me)
            def _():
                copy.wait_send()


def reduce_and_step(grads, weights, m, v, ff, d, count):
    inner = ((2, 4, 16, ff), (4, 2, 16, ff), (4, 80, d))
    half = ((1, 4, 16, ff), (2, 2, 16, ff), (2, 80, d))
    small = ((2, 16, ff), (2, 16, ff), (80, d))
    width = (ff, ff, d)
    whole = ((2, 4, 4, 4, 16, ff), (2, 4, 4, 4, 16, ff), (2, 4, 4, 2, 80, d))

    def vmem(shapes, dtype=BF16):
        return [pltpu.VMEM(s, dtype) for s in shapes]

    three = range(3)
    scratch = (
        vmem((2, 4, *inner[w]) for w in three)
        + vmem((2, 4, *inner[w]) for w in three)
        + vmem((2, 2, *half[w]) for w in three)
        + vmem((2, 2, *inner[w]) for w in three)
        + vmem((2, 3, *small[w]) for w in three)
        + vmem((2, 2, 2, PAD[w], width[w]) for w in three)
        + vmem((2, 4, PAD[w], width[w]) for w in three)
        + vmem(((2, PAD[w], width[w]) for w in three), F32)
        + vmem((2, PAD[w], width[w]) for w in three)
        + vmem((2, 4, PAD[w], width[w]) for w in three)
        + vmem((2, *inner[w]) for w in three)
        + vmem(((80, d), (8, 8, 128), (4, 8, 128), (4, 8, 128)), F32)
        + [pltpu.SemaphoreType.DMA((n,)) for n in (24, 24, 24, 36, 36, 18, 18, 24, 24, 13, 13, 24, 24, 18, 18, 24, 24, 30, 30, 6)]
    )
    in_vmem, anywhere = pl.BlockSpec(memory_space=pltpu.VMEM), pl.BlockSpec(memory_space=pl.ANY)
    moments = [jax.ShapeDtypeStruct(t.shape, F32) for t in m]
    out = pl.pallas_call(
        functools.partial(step_kernel, count),
        out_shape=[jax.ShapeDtypeStruct(s, BF16) for s in whole] + moments + moments,
        in_specs=[anywhere] * 6 + [in_vmem] * 9,
        out_specs=[anywhere] * 3 + [in_vmem] * 6,
        scratch_shapes=scratch,
        compiler_params=pltpu.CompilerParams(collective_id=0, has_side_effects=True, vmem_limit_bytes=66_000_000),
        name="reduce_and_step",
    )(*(g for pair in grads for g in pair), *weights, *m, *v)
    return out[:3], out[3:6], out[6:]


def matmul(a, w):
    return jnp.dot(a, w, preferred_element_type=F32).astype(BF16)


def to_rows(a, b):
    return lax.dot_general(a, b, (((0,), (0,)), ((), ())), preferred_element_type=F32).astype(BF16)


def times_transposed(a, w):
    return lax.dot_general(a, w, (((1,), (1,)), ((), ())), preferred_element_type=F32).astype(BF16)


def normed(h):
    wide = h.astype(F32)
    scale = lax.rsqrt(jnp.mean(wide**2, -1, keepdims=True) + 1e-6)
    return (wide * scale).astype(BF16)


def gated(gate, up):
    return jax.nn.silu(gate) * up


def gradients_of(x, dy, w_gate, w_up, w_down):
    d = x.shape[1]
    column = lax.broadcasted_iota(jnp.int32, (d, d // 7 * 8), 1)
    row = lax.broadcasted_iota(jnp.int32, (d, d // 7 * 8), 0)
    spread = ((row // 7) * 8 + row % 7 == column).astype(BF16)
    layers = w_gate.shape[0]
    h, saved = x, []
    for n in range(layers):
        a = normed(h)
        gate = jnp.dot(a, w_gate[n], preferred_element_type=F32)
        up = jnp.dot(a, w_up[n], preferred_element_type=F32)
        act = gated(gate, up).astype(BF16)
        saved.append((h, a, gate, up, act))
        if n + 1 < layers:
            h = h + matmul(act, w_down[n])
    grads = [None] * layers
    for n in reversed(range(layers)):
        h, a, gate, up, act = saved[n]
        by_act = times_transposed(dy, w_down[n])
        by_down = to_rows(act, dy)
        _, back = jax.vjp(gated, gate, up)
        by_gate, by_up = (t.astype(BF16) for t in back(by_act.astype(F32)))
        a_spread = matmul(a, spread)
        grads[n] = (to_rows(a_spread, by_gate), to_rows(a_spread, by_up), by_down)
        if n:
            by_a = times_transposed(by_gate, w_gate[n]) + times_transposed(by_up, w_up[n])
            _, back = jax.vjp(normed, h)
            dy = dy + back(by_a)[0]
    return [[grads[n][w] for n in range(layers)] for w in range(3)]


def solution(mesh):
    def step(x, dy, *arrays):
        weights, m, v = (arrays[i : i + 3] for i in (0, 3, 6))
        layers, d, ff = weights[0].shape
        me = lax.axis_index("dp")
        rows = [
            lax.dynamic_slice_in_dim(w, me * n, n, axis=1).astype(F32) for w, n in zip(weights, ROWS, strict=True)
        ]
        grads = gradients_of(x[0], dy[0], *weights)
        shapes = ((4, 4, 4, 16, ff), (4, 4, 4, 16, ff), (4, 4, 2, 80, d))
        grads = [[g.reshape(s) for g in pair] for pair, s in zip(grads, shapes, strict=True)]
        count = sum(w.size for w in weights)
        new, m, v = reduce_and_step(grads, rows, m, v, ff, d, count)
        gate, up = (t.reshape(layers, d // 7, 8, ff)[:, :, :7].reshape(layers, d, ff) for t in new[:2])
        return gate, up, new[2].reshape(layers, ff, d), *m, *v

    whole, cut = P(None, None, None), P(None, "dp", None)
    tokens = P(("rep", "dp"), None, None)
    return jax.shard_map(
        step,
        mesh=mesh,
        in_specs=(tokens, tokens, *[whole] * 3, *[cut] * 6),
        out_specs=(*[P("rep", None, None)] * 3, *[P("rep", "dp", None)] * 6),
        check_vma=False,
    )
```

time: 1260 us -> 419 us (0.33)
  blocking collectives: 608 us -> 0 us
  starting transfers between devices: 197 us -> 0 us
  waiting for transfers between devices: 186 us -> 0 us
  Pallas kernels: 0 us -> 165 us
  local copies, waits for them, and re-layouts: 65.1 us -> 86.9 us
  between operations: 18.1 us -> 1.53 us
  other arithmetic: 21.7 us -> 5.22 us
    unnamed x2 -> x0, blocking collectives: 545 us -> none
    unnamed x64 -> x0, starting transfers between devices: 197 us -> none
    reshape x3 -> x0, waiting for transfers between devices: 184 us -> none  [step(): t.reshape(-1, *t.shape[2:])]
    pallas_call x0 -> x1, Pallas kernels: none -> 165 us  [reduce_and_step(): pl.pallas_call(functools.partial(step_kernel, count), out_shape=[jax.Shap...]
    reduce_sum x1 -> x0, blocking collectives: 62.7 us -> none  [of_a_group(): jnp.sum(g * g)]
    unnamed x89 -> x73, local copies, waits for them, and re-layouts: 61.2 us -> 86.9 us
    unnamed x10 -> x5, other arithmetic: 15.2 us -> 0.01 us
    dot_general x15 -> x17, matrix products: 155 us -> 153 us  [the longest x6 59.2 us: to_rows(): lax.dot_general(a, b, (((0,), (0,)), ((), ())), preferred_element_type=F32)]
  transfers between devices with their start and end apart: 67 -> 0, of which waited for: 4 -> 0; matrix products, arithmetic and copies ran while one was open for 5% -> 0% of each run, Pallas kernels for 0% -> 0%
where the time goes in v1:
time: 419 us; the launch traced here: 412 us
  Pallas kernels  165 us (39%)
  matrix products  153 us (37%)
  local copies, waits for them, and re-layouts  86.9 us (21%)
  other arithmetic  5.22 us (1%)
    pallas_call x1, Pallas kernels, reduce_and_step(): pl.pallas_call(functools.partial(step_kernel, count), out_shape=[jax.Shap...  165 us
    unnamed x73, local copies, waits for them, and re-layouts  86.9 us
    dot_general x6, matrix products, to_rows(): lax.dot_general(a, b, (((0,), (0,)), ((), ())), preferred_element_type=F32)  59.2 us
    dot_general x4, matrix products, times_transposed(): lax.dot_general(a, w, (((1,), (1,)), ((), ())), preferred_element_type=F32)  38.7 us
    dot_general x2, matrix products, gradients_of(): up = jnp.dot(a, w_up[n], preferred_element_type=F32)  22.2 us
    dot_general x2, matrix products, gradients_of(): gate = jnp.dot(a, w_gate[n], preferred_element_type=F32)  18.5 us
    dot_general x3, matrix products, matmul(): return jnp.dot(a, w, preferred_element_type=F32).astype(BF16)  14.6 us

profile of v1, /device:TPU:1, one launch (start us, length us, event | category | flops | bytes accessed | tf_op | source)
XLA Modules:
  0.0 412.1 jit_solution(7229437954720554924)
XLA Ops:
  0.7 1.6 copy.36.refs_9_
  2.3 1.6 copy.37.refs_10_
  3.9 1.6 copy.39.refs_12_
  5.5 1.6 copy.40.refs_13_
  7.1 1.6 dynamic-slice_convert_fusion.refs_8_
  8.7 1.6 copy.38.refs_11_
  11.8 1.8 dynamic-slice_convert_fusion.1
  13.6 2.9 copy.34
  17.0 3.8 copy.35
  20.8 4.0 convolution_convert_fusion.9
  24.8 10.7 %fusion.25 = f32[1024,2560]{1,0:T(8,128)} fusion(bf16[2,896,2560]{2,1,0:T(8,128)(2,1)} %param.13, bf16[1,1024,896]{2,1,0:T(8,128)(2,1)S(1)} %copy-done.1, f32[1024]{0:T(1024)S(1)} %add_rsqrt_fusion), kind=kOutput, calls=%fused_computation.45 | convolution fusion | flops 4700372992 | bytes 16912384 | tf_op jit(solution)/shard_map/dot_general | solution.py:428
  35.6 13.5 %multiply_convert_fusion.1 = (bf16[1024,2560]{1,0:T(8,128)(2,1)}, f32[1024,2560]{1,0:T(8,128)}) fusion(f32[1024,2560]{1,0:T(8,128)} %fusion.25, bf16[2,896,2560]{2,1,0:T(8,128)(2,1)} %param.14, bf16[1,1024,896]{2,1,0:T(8,128)(2,1)S(1)} %copy-done.1, f32[1024]{0:T(1024)S(1)} %add_rsqrt_fusion), kind=kOutput, calls=%fused_computation.17 | convolution fusion | flops 4716101632 | bytes 32641024 | tf_op jit(solution)/shard_map/dot_general | solution.py:429
  49.1 7.8 %fusion.41 = (f32[1024]{0:T(1024)S(1)}, bf16[1024,896]{0,1:T(8,128)(2,1)S(1)}) fusion(bf16[1024,2560]{1,0:T(8,128)(2,1)} %get-tuple-element.47, bf16[2,2560,896]{2,1,0:T(8,128)(2,1)S(1)} %bitcast.96, bf16[1,1024,896]{1,2,0:T(8,128)(2,1)S(1)} %copy.34), kind=kOutput, calls=%fused_computation.64 | convolution fusion | flops 4702206976 | bytes 13504512 | tf_op jit(solution)/shard_map/dot_general | solution.py:398
  57.0 2.7 convolution_convert_fusion.8
  59.7 7.7 %fusion.14 = f32[1024,2560]{1,0:T(8,128)S(1)} fusion(bf16[2,896,2560]{2,1,0:T(8,128)(2,1)} %param.13, bf16[1024,896]{0,1:T(8,128)(2,1)S(1)} %get-tuple-element.50, f32[1024]{0:T(1024)S(1)} %fusion.68), kind=kOutput, calls=%fused_computation.34 | convolution fusion | flops 4700372992 | bytes 16912384 | tf_op jit(solution)/shard_map/dot_general | solution.py:428
  67.5 8.7 %fusion.18 = f32[1024,2560]{1,0:T(8,128)} fusion(bf16[2,896,2560]{2,1,0:T(8,128)(2,1)S(1)} %bitcast.100, bf16[1024,896]{0,1:T(8,128)(2,1)S(1)} %get-tuple-element.50, f32[1024]{0:T(1024)S(1)} %fusion.68), kind=kOutput, calls=%fused_computation.38 | convolution fusion | flops 4700372992 | bytes 16912384 | tf_op jit(solution)/shard_map/dot_general | solution.py:429
  76.3 10.2 %convolution_convert_fusion.6 = bf16[2560,896]{1,0:T(8,128)(2,1)} fusion(f32[1024,2560]{1,0:T(8,128)} %fusion.18, bf16[1,1024,896]{2,1,0:T(8,128)(2,1)S(1)} %copy-done.2, f32[1024,2560]{1,0:T(8,128)S(1)} %fusion.14), kind=kOutput, calls=%fused_computation.30 | convolution fusion | flops 4715642880 | bytes 27394048 | tf_op jit(solution)/shard_map/dot_general | solution.py:402
  86.5 17.2 %fusion = (bf16[1024,2560]{1,0:T(8,128)(2,1)}, bf16[1024,2560]{1,0:T(8,128)(2,1)}) fusion(f32[1024,2560]{1,0:T(8,128)} %copy-done.9, f32[1024,2560]{1,0:T(8,128)} %fusion.18, bf16[2,2560,896]{2,1,0:T(8,128)(2,1)} %param.15, bf16[1,1024,896]{2,1,0:T(8,128)(2,1)S(1)} %copy-done.2), kind=kOutput, calls=%fused_computation.6 | convolution fusion | flops 4739563520 | bytes 37879808 | tf_op jit(solution)/shard_map/dot_general | solution.py:406
  103.7 8.9 %fusion.12 = bf16[1024,896]{0,1:T(8,128)(2,1)S(1)} fusion(bf16[1024,2560]{1,0:T(8,128)(2,1)} %get-tuple-element.46, bf16[2,896,2560]{2,1,0:T(8,128)(2,1)} %param.13), kind=kOutput, calls=%fused_computation.32 | convolution fusion | flops 4697620480 | bytes 11665408 | tf_op jit(solution)/shard_map/dot_general | solution.py:406
  112.7 10.2 %convolution_convert_fusion.4 = bf16[1024,2560]{1,0:T(8,128)(2,1)} fusion(bf16[1024,1024]{1,0:T(8,128)(2,1)S(1)} %convolution_convert_fusion.8, bf16[1024,2560]{1,0:T(8,128)(2,1)} %get-tuple-element.46), kind=kOutput, calls=%fused_computation.28 | convolution fusion | flops 5371330560 | bytes 12582912 | tf_op jit(solution)/shard_map/dot_general | solution.py:402
  122.9 5.2 %fusion.43 = (f32[1024]{0:T(1024)S(1)}, bf16[1024,896]{0,1:T(8,128)(2,1)S(1)}) fusion(bf16[1024,896]{0,1:T(8,128)(2,1)S(1)} %get-tuple-element.50, bf16[1024,896]{0,1:T(8,128)(2,1)S(1)} %fusion.12, bf16[1024,2560]{1,0:T(8,128)(2,1)S(1)} %copy-done.10, bf16[2,896,2560]{2,1,0:T(8,128)(2,1)S(1)} %bitcast.102), kind=kOutput, calls=%fused_computation.66 | convolution fusion | flops 4703124480 | bytes 15339520 | tf_op jit(solution)/shard_map/dot_general | solution.py:406
  128.0 7.5 %convolution_convert_fusion.2 = bf16[1024,2560]{1,0:T(8,128)(2,1)} fusion(bf16[1024,1024]{1,0:T(8,128)(2,1)S(1)} %convolution_convert_fusion.8, bf16[1024,2560]{1,0:T(8,128)(2,1)S(1)} %copy-done.10), kind=kOutput, calls=%fused_computation.26 | convolution fusion | flops 5371330560 | bytes 12582912 | tf_op jit(solution)/shard_map/dot_general | solution.py:402
  137.0 10.1 %convolution_convert_fusion.7 = bf16[2560,896]{1,0:T(8,128)(2,1)} fusion(bf16[1024,2560]{1,0:T(8,128)(2,1)} %get-tuple-element.47, bf16[1024,896]{0,1:T(8,128)(2,1)S(1)} %fusion.45), kind=kOutput, calls=%fused_computation.31 | convolution fusion | flops 4699914240 | bytes 11665408 | tf_op jit(solution)/shard_map/dot_general | solution.py:402
  147.1 7.4 %convolution_convert_fusion = bf16[1024,2560]{1,0:T(8,128)(2,1)} fusion(bf16[1024,896]{0,1:T(8,128)(2,1)S(1)} %fusion.45, bf16[2,2560,896]{2,1,0:T(8,128)(2,1)S(1)} %bitcast.98), kind=kOutput, calls=%fused_computation.24 | convolution fusion | flops 4700241920 | bytes 11665408 | tf_op jit(solution)/shard_map/dot_general | solution.py:406
  154.5 11.4 %convolution_convert_fusion.5 = bf16[1024,2560]{1,0:T(8,128)(2,1)} fusion(bf16[1024,1024]{1,0:T(8,128)(2,1)S(1)} %copy-done.11, f32[1024,2560]{1,0:T(8,128)S(1)} %bitcast.104, f32[1024,2560]{1,0:T(8,128)} %get-tuple-element.48, bf16[1024,2560]{1,0:T(8,128)(2,1)} %convolution_convert_fusion), kind=kOutput, calls=%fused_computation.29 | convolution fusion | flops 5402787840 | bytes 33554432 | tf_op jit(solution)/shard_map/dot_general | solution.py:402
  166.0 9.7 %convolution_convert_fusion.3 = bf16[1024,2560]{1,0:T(8,128)(2,1)} fusion(bf16[1024,1024]{1,0:T(8,128)(2,1)S(1)} %copy-done.11, bf16[1024,2560]{1,0:T(8,128)(2,1)} %convolution_convert_fusion, f32[1024,2560]{1,0:T(8,128)S(1)} %bitcast.104), kind=kOutput, calls=%fused_computation.27 | convolution fusion | flops 5389680640 | bytes 23068672 | tf_op jit(solution)/shard_map/dot_general | solution.py:402
  175.7 165.4 %reduce_and_step.1 = (bf16[2,4,4,4,16,2560]{5,4,3,2,1,0:T(8,128)(2,1)}, bf16[2,4,4,4,16,2560]{5,4,3,2,1,0:T(8,128)(2,1)}, bf16[2,4,4,2,80,896]{5,4,3,2,1,0:T(8,1...) custom-call(bf16[4,4,4,16,2560]{4,3,2,1,0:T(8,128)(2,1)} %bitcast.91, ...), custom_call_target="tpu_custom_call" | custom-call | tf_op jit(solution)/shard_map/reduce_and_step/pallas_call | solution.py:385
  341.1 20.4 %copy.52 = bf16[2,128,7,2560]{3,0,2,1:T(2,128)(2,1)} copy(bf16[2,128,7,2560]{3,2,1,0:T(8,128)(2,1)} %bitcast.87) | data formatting | bytes 18350080
  361.5 8.7 %copy.44 = bf16[2,896,2560]{2,1,0:T(8,128)(2,1)} copy(bf16[2,896,2560]{2,0,1:T(2,128)(2,1)} %bitcast.84) | data formatting | bytes 18350080
  370.2 20.1 %copy.53 = bf16[2,128,7,2560]{3,0,2,1:T(2,128)(2,1)} copy(bf16[2,128,7,2560]{3,2,1,0:T(8,128)(2,1)} %bitcast.86) | data formatting | bytes 18350080
  390.3 8.8 %copy.45 = bf16[2,896,2560]{2,1,0:T(8,128)(2,1)} copy(bf16[2,896,2560]{2,0,1:T(2,128)(2,1)} %bitcast.85) | data formatting | bytes 18350080
  403.7 8.0 %copy.55 = bf16[2,2560,896]{2,1,0:T(8,128)(2,1)} copy(bf16[2,2560,896]{2,1,0:T(8,128)(2,1)} %bitcast.88) | data formatting | bytes 18350080
  (74 shorter events, 8.1 us)
Async XLA Ops:
  20.8 4.0 copy-start.1
  24.8 24.2 %slice-start = ((s8[9175040]{0:T(1024)(128)(4,1)}), s8[4194304]{0:T(1024)(128)(4,1)S(1)}, s32[]{:S(2)}) async-start(s8[9175040]{0:T(1024)(128)(4,1)} %bitcast.95), calls=%async_computation | async-start | bytes 8388608
  35.6 13.5 %slice-start.1 = ((s8[9175040]{0:T(1024)(128)(4,1)}), s8[4194304]{0:T(1024)(128)(4,1)S(1)}, s32[]{:S(2)}) async-start(s8[9175040]{0:T(1024)(128)(4,1)} %bitcast.95), calls=%async_computation.1 | async-start | bytes 8388608
  35.6 13.5 %slice-start.2 = ((s8[9175040]{0:T(1024)(128)(4,1)}), s8[786432]{0:T(1024)(128)(4,1)S(1)}, s32[]{:S(2)}) async-start(s8[9175040]{0:T(1024)(128)(4,1)} %bitcast.95), calls=%async_computation.2 | async-start | bytes 1572864
  57.0 10.5 %slice-start.6 = ((s8[9175040]{0:T(1024)(128)(4,1)}), s8[4194304]{0:T(1024)(128)(4,1)S(1)}, s32[]{:S(2)}) async-start(s8[9175040]{0:T(1024)(128)(4,1)} %bitcast.99), calls=%async_computation.6 | async-start | bytes 8388608
  57.0 10.5 %slice-start.7 = ((s8[9175040]{0:T(1024)(128)(4,1)}), s8[4194304]{0:T(1024)(128)(4,1)S(1)}, s32[]{:S(2)}) async-start(s8[9175040]{0:T(1024)(128)(4,1)} %bitcast.99), calls=%async_computation.7 | async-start | bytes 8388608
  59.7 7.8 %slice-start.8 = ((s8[9175040]{0:T(1024)(128)(4,1)}), s8[786432]{0:T(1024)(128)(4,1)S(1)}, s32[]{:S(2)}) async-start(s8[9175040]{0:T(1024)(128)(4,1)} %bitcast.99), calls=%async_computation.8 | async-start | bytes 1572864
  67.5 8.8 %copy-start.9 = (f32[1024,2560]{1,0:T(8,128)}, f32[1024,2560]{1,0:T(8,128)S(1)}, u32[]{:S(2)}) copy-start(f32[1024,2560]{1,0:T(8,128)S(1)} %fusion.14) | copy-start | bytes 31457284
  67.5 8.8 %copy-start.2 = (bf16[1,1024,896]{2,1,0:T(8,128)(2,1)S(1)}, bf16[1,1024,896]{2,1,0:T(8,128)(2,1)}, u32[]{:S(2)}) copy-start(bf16[1,1024,896]{2,1,0:T(8,128)(2,1)} %param.12) | copy-start | bytes 5505028
  103.7 19.1 %slice-start.9 = ((s8[9175040]{0:T(1024)(128)(4,1)}), s8[4194304]{0:T(1024)(128)(4,1)S(1)}, s32[]{:S(2)}) async-start(s8[9175040]{0:T(1024)(128)(4,1)} %bitcast.101), calls=%async_computation.9 | async-start | bytes 8388608
  103.7 19.1 %slice-start.10 = ((s8[9175040]{0:T(1024)(128)(4,1)}), s8[4194304]{0:T(1024)(128)(4,1)S(1)}, s32[]{:S(2)}) async-start(s8[9175040]{0:T(1024)(128)(4,1)} %bitcast.101), calls=%async_computation.10 | async-start | bytes 8388608
  112.7 10.2 %slice-start.11 = ((s8[9175040]{0:T(1024)(128)(4,1)}), s8[786432]{0:T(1024)(128)(4,1)S(1)}, s32[]{:S(2)}) async-start(s8[9175040]{0:T(1024)(128)(4,1)} %bitcast.101), calls=%async_computation.11 | async-start | bytes 1572864
  112.7 10.2 %copy-start.10 = (bf16[1024,2560]{1,0:T(8,128)(2,1)S(1)}, bf16[1024,2560]{1,0:T(8,128)(2,1)}, u32[]{:S(2)}) copy-start(bf16[1024,2560]{1,0:T(8,128)(2,1)} %get-tuple-element.45) | copy-start | bytes 15728644
  128.0 7.5 %copy-start = (bf16[1,1024,896]{1,2,0:T(8,128)(2,1)S(1)}, bf16[1,1024,896]{1,2,0:T(8,128)(2,1)}, u32[]{:S(2)}) copy-start(bf16[1,1024,896]{1,2,0:T(8,128)(2,1)} %copy.35) | copy-start | bytes 5505028
  135.6 11.5 %slice-start.3 = ((s8[9175040]{0:T(1024)(128)(4,1)}), s8[786432]{0:T(1024)(128)(4,1)S(1)}, s32[]{:S(2)}) async-start(s8[9175040]{0:T(1024)(128)(4,1)} %bitcast.97), calls=%async_computation.3 | async-start | bytes 1572864
  136.9 10.2 %slice-start.4 = ((s8[9175040]{0:T(1024)(128)(4,1)}), s8[4194304]{0:T(1024)(128)(4,1)S(1)}, s32[]{:S(2)}) async-start(s8[9175040]{0:T(1024)(128)(4,1)} %bitcast.97), calls=%async_computation.4 | async-start | bytes 8388608
  136.9 10.1 %slice-start.5 = ((s8[9175040]{0:T(1024)(128)(4,1)}), s8[4194304]{0:T(1024)(128)(4,1)S(1)}, s32[]{:S(2)}) async-start(s8[9175040]{0:T(1024)(128)(4,1)} %bitcast.97), calls=%async_computation.5 | async-start | bytes 8388608
  137.0 17.5 %slice-start.12 = ((s8[10485760]{0:T(1024)(128)(4,1)}), s8[4194304]{0:T(1024)(128)(4,1)S(1)}, s32[]{:S(2)}) async-start(s8[10485760]{0:T(1024)(128)(4,1)} %bitcast.103), calls=%async_computation.12 | async-start | bytes 8388608
  137.0 17.5 %slice-start.13 = ((s8[10485760]{0:T(1024)(128)(4,1)}), s8[4194304]{0:T(1024)(128)(4,1)S(1)}, s32[]{:S(2)}) async-start(s8[10485760]{0:T(1024)(128)(4,1)} %bitcast.103), calls=%async_computation.13 | async-start | bytes 8388608
  147.1 7.4 %slice-start.14 = ((s8[10485760]{0:T(1024)(128)(4,1)}), s8[2097152]{0:T(1024)(128)(4,1)S(1)}, s32[]{:S(2)}) async-start(s8[10485760]{0:T(1024)(128)(4,1)} %bitcast.103), calls=%async_computation.14 | async-start | bytes 4194304
  147.1 7.4 %copy-start.11 = (bf16[1024,1024]{1,0:T(8,128)(2,1)S(1)}, bf16[1024,1024]{1,0:T(8,128)(2,1)}, u32[]{:S(2)}) copy-start(bf16[1024,1024]{1,0:T(8,128)(2,1)} %convolution_convert_fusion.9) | copy-start | bytes 6291460
  390.3 8.8 %copy-start.8 = (f32[2,7,2560]{2,1,0:T(8,128)S(1)}, f32[2,7,2560]{2,1,0:T(8,128)}, u32[]{:S(2)}) copy-start(f32[2,7,2560]{2,1,0:T(8,128)} %get-tuple-element.39) | copy-start | bytes 430084
  390.3 9.6 %copy-start.7 = (f32[2,7,2560]{2,1,0:T(8,128)S(1)}, f32[2,7,2560]{2,1,0:T(8,128)}, u32[]{:S(2)}) copy-start(f32[2,7,2560]{2,1,0:T(8,128)} %get-tuple-element.40) | copy-start | bytes 430084
  390.3 10.4 %copy-start.4 = (f32[2,20,896]{2,1,0:T(8,128)S(1)}, f32[2,20,896]{2,1,0:T(8,128)}, u32[]{:S(2)}) copy-start(f32[2,20,896]{2,1,0:T(8,128)} %get-tuple-element.41) | copy-start | bytes 430084
  390.3 11.1 %copy-start.6 = (f32[2,7,2560]{2,1,0:T(8,128)S(1)}, f32[2,7,2560]{2,1,0:T(8,128)}, u32[]{:S(2)}) copy-start(f32[2,7,2560]{2,1,0:T(8,128)} %get-tuple-element.42) | copy-start | bytes 430084
  390.3 11.8 %copy-start.5 = (f32[2,7,2560]{2,1,0:T(8,128)S(1)}, f32[2,7,2560]{2,1,0:T(8,128)}, u32[]{:S(2)}) copy-start(f32[2,7,2560]{2,1,0:T(8,128)} %get-tuple-element.43) | copy-start | bytes 430084
  390.3 12.6 %copy-start.3 = (f32[2,20,896]{2,1,0:T(8,128)S(1)}, f32[2,20,896]{2,1,0:T(8,128)}, u32[]{:S(2)}) copy-start(f32[2,20,896]{2,1,0:T(8,128)} %get-tuple-element.44) | copy-start | bytes 430084
